TPU v7x, 32 devices: a whole 2x2x4 slice. The times are simulated.
32 devices in a mesh: group: 2 (over x), patch: 16 (over z, y, core).
Axes of the slice: x: 2, y: 2, z: 4, core: 2. Of those that a mesh axis runs over, the one named last changes fastest.
Arguments:
- features: bfloat16 [32, 64, 4, 2304], P(('group', 'patch')), parts along dimension 0, may hold values from -6 to 6
- w_in: bfloat16 [28, 64], replicated, may hold values from -0.75 to 0.75
- w_plane: bfloat16 [9, 28, 28], replicated, may hold values from -0.375 to 0.375
- w_depth: bfloat16 [3, 28, 28], replicated, may hold values from -0.625 to 0.625
- w_head: bfloat16 [3, 28], replicated, may hold values from -1 to 1
- brick_owner: int32 [32], P(('group', 'patch')), parts along dimension 0, may hold values from 0 to 15, each once
- patch_anchor: int32 [32], P(('group', 'patch')), parts along dimension 0, may hold values from 0 to 3, as said below
- aug_code: int32 [32], P(('group', 'patch')), parts along dimension 0, may hold values from 0 to 7, as said below
Outputs:
- blended: float32 [32, 4, 2304], P(('group', 'patch')), parts along dimension 0
There are 2 independent parts, one for each index of `group`. A program takes and returns all parts, laid end to end along the dimension named above; an argument that names none is the same for every part. Nothing has to cross between parts.
Inputs may be any that keep to these rules, and one draw needn't show every extreme that they name: `brick_owner`: every device owns exactly one brick of its region. `patch_anchor`: devices 8 k to 8 k + 7 share one anchor; different positions have different anchors. `aug_code`: devices 8 k to 8 k + 7 hold each code once.
All inputs are finite; a program needn't handle non-finite values.
Results may differ from a plain program's by a relative error of at most 0.00048.
Values sent between devices are 32-bit elements; how exact they have to be, the bound alone decides.
No kernel may reach another device: no remote copies, remote signals or barrier semaphores. Data moves between devices by JAX's collectives and lax.ppermute only.
A program may use at most 64 MiB of HBM per device.

v0:
```python
import math

import jax
import jax.numpy as jnp
from jax import lax
from jax.sharding import PartitionSpec as P


def bump_curve(length):
    position = (jnp.arange(length, dtype=jnp.float32) + 0.5) / length
    return 0.1 + jnp.sin(jnp.pi * position) ** 2


def window_volume(patch_depth, plane_side):
    return (
        bump_curve(patch_depth)[:, None, None]
        * bump_curve(plane_side)[None, :, None]
        * bump_curve(plane_side)[None, None, :]
    )


def brick_partition(volume, brick_side):
    channels, patch_depth = (volume.shape[0], volume.shape[1])
    blocks = volume.reshape(channels, patch_depth, 4, brick_side, 4, brick_side).transpose(
        2, 4, 0, 1, 3, 5
    )
    return blocks.reshape(16, channels, patch_depth * brick_side * brick_side)


def plane_shift(values, offset, plane_side):
    length = values.shape[2]
    margin = plane_side + 1
    padded = jnp.pad(values, ((0, 0), (0, 0), (margin, margin)))
    return lax.slice_in_dim(padded, margin + offset, margin + offset + length, axis=2)


def patch_output(patch_feat, flip_code, w_in, w_plane, w_depth, w_head):
    channels, patch_depth, half_plane = patch_feat.shape
    half_side = math.isqrt(half_plane)
    plane_side = 2 * half_side
    brick_side = plane_side // 4
    hidden = w_in.shape[0]
    projected = jnp.einsum(
        "oi,izp->ozp", w_in, patch_feat, preferred_element_type=jnp.float32
    ).astype(jnp.bfloat16)
    coarse_grid = projected.reshape(hidden, patch_depth, half_side, 1, half_side, 1)
    upsampled = jnp.broadcast_to(coarse_grid, (hidden, patch_depth, half_side, 2, half_side, 2))
    upsampled = upsampled.reshape(hidden, patch_depth, plane_side * plane_side)
    columns = jnp.arange(plane_side * plane_side, dtype=jnp.int32) % plane_side
    edge_masks = (
        (columns >= 1).astype(jnp.bfloat16),
        None,
        (columns <= plane_side - 2).astype(jnp.bfloat16),
    )
    mix_total = jnp.zeros((hidden, patch_depth, plane_side * plane_side), jnp.float32)
    for row_tap in range(3):
        for col_tap in range(3):
            shifted_in = plane_shift(
                upsampled, (row_tap - 1) * plane_side + col_tap - 1, plane_side
            )
            if col_tap != 1:
                shifted_in = shifted_in * edge_masks[col_tap]
            mix_total = mix_total + jnp.einsum(
                "oi,izp->ozp",
                w_plane[3 * row_tap + col_tap],
                shifted_in,
                preferred_element_type=jnp.float32,
            )
    first_out = (upsampled.astype(jnp.float32) + jax.nn.relu(mix_total)).astype(jnp.bfloat16)
    padded_depth = jnp.pad(first_out, ((0, 0), (1, 1), (0, 0)))
    mix_total = jnp.zeros((hidden, patch_depth, plane_side * plane_side), jnp.float32)
    for depth_tap in range(3):
        mix_total = mix_total + jnp.einsum(
            "oi,izp->ozp",
            w_depth[depth_tap],
            padded_depth[:, depth_tap : depth_tap + patch_depth],
            preferred_element_type=jnp.float32,
        )
    second_out = (first_out.astype(jnp.float32) + jax.nn.relu(mix_total)).astype(jnp.bfloat16)
    logits = jnp.einsum("oi,izp->ozp", w_head, second_out, preferred_element_type=jnp.float32)
    affinity = jax.nn.sigmoid(logits).reshape(3, patch_depth, plane_side, plane_side)
    affinity = jnp.where(flip_code % 2 == 1, affinity[:, ::-1], affinity)
    affinity = jnp.where(flip_code // 2 % 2 == 1, affinity[:, :, ::-1], affinity)
    affinity = jnp.where(flip_code // 4 % 2 == 1, affinity[:, :, :, ::-1], affinity)
    window = window_volume(patch_depth, plane_side)
    weighted = affinity * window[None]
    weighted = jnp.concatenate([weighted, window[None]], axis=0)
    return (brick_partition(weighted, brick_side), window)


def on_device(features, w_in, w_plane, w_depth, w_head, brick_owner, patch_anchor, aug_code):
    devices = lax.axis_size("patch")
    brick_rows = devices // 4
    owner_lookup = lax.all_gather(brick_owner, "patch", axis=0, tiled=True)
    volume_bricks, window = patch_output(features[0], aug_code[0], w_in, w_plane, w_depth, w_head)
    tile_index = jnp.arange(16, dtype=jnp.int32)
    device_ids = jnp.arange(devices, dtype=jnp.int32)
    brick_id = (patch_anchor[0] + tile_index // 4) % brick_rows * 4 + tile_index % 4
    table_hits = brick_id[:, None] == device_ids[None, :]
    owners = jnp.sum(jnp.where(table_hits, owner_lookup[None, :], 0), axis=1)
    delivery_routes = (owners[None, :] == device_ids[:, None]).astype(jnp.float32)
    departing_pieces = jnp.einsum(
        "ve,eig->vig", delivery_routes, volume_bricks, precision=lax.Precision.HIGHEST
    )
    received = lax.all_to_all(departing_pieces, "patch", split_axis=0, concat_axis=0, tiled=True)
    arrived = jnp.sum(received, axis=0, keepdims=True)
    return arrived


def solution(mesh):
    in_specs = (
        P(("group", "patch"), None, None, None),
        P(),
        P(),
        P(),
        P(),
        P(("group", "patch")),
        P(("group", "patch")),
        P(("group", "patch")),
    )
    out_specs = P(("group", "patch"), None, None)
    return jax.shard_map(
        on_device, mesh=mesh, in_specs=in_specs, out_specs=out_specs, check_vma=False
    )
```

profile of v0, /device:TPU:0, one launch (start us, length us, event | category | flops | bytes accessed | tf_op | source)
XLA Modules:
  0.0 95.0 jit_solution(16755403858895298420)
XLA Ops:
  0.0 0.0 copy-start
  0.0 0.6 fusion.46
  0.6 0.6 fusion.47
  2.1 0.1 multiply_add_fusion
  2.1 0.0 copy-done
  2.2 1.8 %convolution_convert_fusion = bf16[28,4,2304]{2,0,1:T(8,128)(2,1)} fusion(bf16[64,4,2304]{2,1,0:T(4,128)(2,1)S(1)} %bitcast.99, bf16[28,64]{1,0:T(8,128)(2,1)} %param.9), kind=kOutput, calls=%fused_computation.23 | convolution fusion | flops 33288192 | bytes 1699328 | tf_op jit(solution)/shard_map/oi,izp->ozp/dot_general | solution.py:43
  4.0 2.1 %copy.40 = bf16[28,4,2304]{0,2,1:T(8,128)(2,1)S(1)} copy(bf16[28,4,2304]{2,0,1:T(8,128)(2,1)} %convolution_convert_fusion) | data formatting | bytes 1032192 | tf_op jit(solution)/shard_map/broadcast_in_dim | solution.py:47
  6.0 7.1 %broadcast_in_dim.17 = bf16[28,4,48,2,48,2]{0,5,4,3,2,1:T(2,128)(2,1)} broadcast(bf16[28,4,48,48]{0,3,2,1:T(8,128)(2,1)S(1)} %bitcast.104), dimensions={0,1,2,4} | broadcast | bytes 2580480 | tf_op jit(solution)/shard_map/broadcast_in_dim | solution.py:47
  13.1 0.0 copy-start.3
  13.1 0.0 copy-start.5
  13.1 7.5 %copy.31 = bf16[28,4,9216]{2,0,1:T(8,128)(2,1)S(1)} copy(bf16[28,4,9216]{0,2,1:T(8,128)(2,1)} %bitcast.100) | data formatting | bytes 4128768 | tf_op jit(solution)/shard_map/reshape | solution.py:48
  20.7 0.0 copy-done.3
  20.7 0.0 copy-done.5
  20.7 1.1 %fusion.24 = f32[4,9216,28]{1,2,0:T(8,128)S(1)} fusion(bf16[9216]{0:T(1024)(128)(2,1)S(1)} %copy-done.3, bf16[28,4,9216]{2,0,1:T(8,128)(2,1)S(1)} %copy.31, bf16[9,28,28]{2,1,0:T(8,128)(2,1)S(1)} %copy-done.5), kind=kOutput, calls=%fused_computation.37 | convolution fusion | flops 61931520 | bytes 6514688 | tf_op jit(solution)/shard_map/oi,izp->ozp/dot_general | solution.py:63
  21.8 0.0 copy-start.4
  21.8 1.3 %convolution_add_fusion.9 = f32[4,9216,28]{1,2,0:T(8,128)S(1)} fusion(f32[4,9216,28]{1,2,0:T(8,128)S(1)} %fusion.24, bf16[28,4,9216]{2,0,1:T(8,128)(2,1)S(1)} %copy.31, bf16[9,28,28]{2,1,0:T(8,128)(2,1)S(1)} %copy-done.5), kind=kOutput, calls=%fused_computation.15 | convolution fusion | flops 58834944 | bytes 11214848 | tf_op jit(solution)/shard_map/oi,izp->ozp/dot_general | solution.py:63
  23.1 0.0 copy-done.4
  23.1 0.0 slice-start
  23.1 0.0 slice-start.1
  23.1 1.4 %convolution_add_fusion.8 = f32[4,9216,28]{1,2,0:T(8,128)S(1)} fusion(f32[4,9216,28]{1,2,0:T(8,128)S(1)} %convolution_add_fusion.9, bf16[9216]{0:T(1024)(128)(2,1)S(1)} %copy-done.4, bf16[28,4,9216]{2,0,1:T(8,128)(2,1)S(1)} %copy.31, bf16[9,28,28]{2,1,0:T(8,128)(2,1)S(1)} %copy-done.5), kind=kOutput, calls=%fused_computation.14 | convolution fusion | flops 62963712 | bytes 11233280 | tf_op jit(solution)/shard_map/oi,izp->ozp/dot_general | solution.py:63
  24.6 0.0 slice-start.2
  24.6 1.4 %convolution_add_fusion.7 = f32[4,9216,28]{1,2,0:T(8,128)S(1)} fusion(f32[4,9216,28]{1,2,0:T(8,128)S(1)} %convolution_add_fusion.8, bf16[9216]{0:T(1024)(128)(2,1)S(1)} %copy-done.3, bf16[28,4,9216]{2,0,1:T(8,128)(2,1)S(1)} %copy.31, bf16[9,28,28]{2,1,0:T(8,128)(2,1)S(1)} %copy-done.5), kind=kOutput, calls=%fused_computation.13 | convolution fusion | flops 62963712 | bytes 11233280 | tf_op jit(solution)/shard_map/oi,izp->ozp/dot_general | solution.py:63
  26.0 0.0 slice-done
  26.0 0.6 slice-done.1
  26.6 0.4 slice-done.2
  27.0 3.4 %convolution_add_fusion.6 = f32[4,9216,28]{1,2,0:T(8,128)S(1)} fusion(f32[4,9216,28]{1,2,0:T(8,128)S(1)} %convolution_add_fusion.7, bf16[28,4,9216]{0,2,1:T(8,128)(2,1)S(1)} %bitcast.103, bf16[9,28,28]{2,1,0:T(8,128)(2,1)S(1)} %copy-done.5), kind=kOutput, calls=%fused_computation.12 | convolution fusion | flops 58834944 | bytes 18292736 | tf_op jit(solution)/shard_map/oi,izp->ozp/dot_general | solution.py:63
  30.4 1.4 %convolution_add_fusion.5 = f32[4,9216,28]{1,2,0:T(8,128)S(1)} fusion(f32[4,9216,28]{1,2,0:T(8,128)S(1)} %convolution_add_fusion.6, bf16[9216]{0:T(1024)(128)(2,1)S(1)} %copy-done.4, bf16[28,4,9216]{2,0,1:T(8,128)(2,1)S(1)} %copy.31, bf16[9,28,28]{2,1,0:T(8,128)(2,1)S(1)} %copy-done.5), kind=kOutput, calls=%fused_computation.11 | convolution fusion | flops 62963712 | bytes 11233280 | tf_op jit(solution)/shard_map/oi,izp->ozp/dot_general | solution.py:63
  31.8 1.4 %convolution_add_fusion.4 = f32[4,9216,28]{1,2,0:T(8,128)S(1)} fusion(f32[4,9216,28]{1,2,0:T(8,128)S(1)} %convolution_add_fusion.5, bf16[9216]{0:T(1024)(128)(2,1)S(1)} %copy-done.3, bf16[28,4,9216]{2,0,1:T(8,128)(2,1)S(1)} %copy.31, bf16[9,28,28]{2,1,0:T(8,128)(2,1)S(1)} %copy-done.5), kind=kOutput, calls=%fused_computation.10 | convolution fusion | flops 62963712 | bytes 11233280 | tf_op jit(solution)/shard_map/oi,izp->ozp/dot_general | solution.py:63
  33.2 1.3 %convolution_add_fusion.3 = f32[4,9216,28]{1,2,0:T(8,128)S(1)} fusion(f32[4,9216,28]{1,2,0:T(8,128)S(1)} %convolution_add_fusion.4, bf16[28,4,9216]{2,0,1:T(8,128)(2,1)S(1)} %copy.31, bf16[9,28,28]{2,1,0:T(8,128)(2,1)S(1)} %copy-done.5), kind=kOutput, calls=%fused_computation.9 | convolution fusion | flops 58834944 | bytes 11214848 | tf_op jit(solution)/shard_map/oi,izp->ozp/dot_general | solution.py:63
  34.5 0.0 copy-start.6
  34.5 1.9 %fusion.6 = bf16[28,4,9216]{2,0,1:T(8,128)(2,1)S(1)} fusion(f32[4,9216,28]{1,2,0:T(8,128)S(1)} %convolution_add_fusion.3, bf16[28,4,9216]{2,0,1:T(8,128)(2,1)S(1)} %copy.31, bf16[9216]{0:T(1024)(128)(2,1)S(1)} %copy-done.4, bf16[9,28,28]{2,1,0:T(8,128)(2,1)S(1)} %copy-done.5), kind=kOutput, calls=%fused_computation.16 | convolution fusion | flops 67092480 | bytes 11528192 | tf_op jit(solution)/shard_map/oi,izp->ozp/dot_general | solution.py:63
  36.4 0.0 copy-done.6
  36.4 0.0 copy-start.2
  36.4 1.0 %fusion.51 = f32[4,9216,28]{1,2,0:T(8,128)S(1)} fusion(bf16[28,4,9216]{2,0,1:T(8,128)(2,1)S(1)} %fusion.6, bf16[3,28,28]{2,1,0:T(8,128)(2,1)S(1)} %copy-done.6), kind=kOutput, calls=%fused_computation.70 | convolution fusion | flops 57802752 | bytes 6496256 | tf_op jit(solution)/shard_map/oi,izp->ozp/dot_general | solution.py:73
  37.4 0.5 copy-done.2
  37.8 0.0 copy-start.7
  37.8 3.1 %convolution_add_fusion.1 = f32[4,9216,28]{1,2,0:T(8,128)} fusion(f32[4,9216,28]{1,2,0:T(8,128)S(1)} %fusion.51, bf16[28,4,9216]{2,0,1:T(8,128)(2,1)S(1)} %fusion.6, bf16[3,28,28]{2,1,0:T(8,128)(2,1)S(1)} %copy-done.6), kind=kOutput, calls=%fused_computation.4 | convolution fusion | flops 44384256 | bytes 11214848 | tf_op jit(solution)/shard_map/oi,izp->ozp/dot_general | solution.py:73
  40.9 0.0 copy-done.7
  40.9 4.8 %fusion.11 = f32[3,4,9216]{2,0,1:T(4,128)S(1)} fusion(f32[4,9216,28]{1,2,0:T(8,128)} %convolution_add_fusion.1, bf16[28,4,9216]{2,0,1:T(8,128)(2,1)} %copy-done.2, bf16[3,28,28]{2,1,0:T(8,128)(2,1)S(1)} %copy-done.6, bf16[3,28]{1,0:T(4,128)(2,1)S(1)} %copy-done.7), kind=kOutput, calls=%fused_computation.22 | convolution fusion | flops 55037952 | bytes 9888768 | tf_op jit(solution)/shard_map/oi,izp->ozp/dot_general | solution.py:80
  45.7 0.3 copy.34
  46.0 0.3 reshape.138
  46.4 0.3 rev.10
  46.8 0.1 broadcast_select_fusion
  46.9 1.0 %rev.11 = f32[3,4,96,96]{3,2,1,0:T(8,128)S(1)} reverse(f32[3,4,96,96]{3,2,1,0:T(8,128)S(1)} %broadcast_select_fusion), dimensions={3} | reverse | bytes 884736 | tf_op jit(solution)/shard_map/rev | solution.py:84
  47.9 0.1 broadcast_multiply_fusion.3
  47.9 0.1 broadcast_multiply_fusion.1
  48.1 0.9 select_multiply_fusion
  49.0 2.2 %concatenate.6 = f32[3,4,4,24,4,24]{5,4,3,2,1,0:T(4,128)S(1)} reshape(f32[3,4,96,96]{3,2,1,0:T(8,128)} %select_multiply_fusion) | data formatting | bytes 884736 | tf_op jit(solution)/shard_map/concatenate | solution.py:87
  51.2 0.3 copy.35
  51.5 0.1 broadcast_multiply_fusion.2
  51.5 0.2 broadcast_multiply_fusion
  52.4 0.0 copy-start.8
  52.4 1.9 %maximum_bitcast_fusion = f32[4,4,4,4,24,24]{5,4,3,1,0,2:T(8,128)} fusion(f32[1,4,4,24,4,24]{5,3,1,4,2,0:T(8,128)S(1)} %broadcast_multiply_fusion, f32[3,4,4,24,4,24]{5,3,1,4,2,0:T(8,128)S(1)} %copy.35), kind=kLoop, calls=%fused_computation.24 | loop fusion | flops 147456 | bytes 1179648 | tf_op jit(solution)/shard_map/transpose | solution.py:24
  54.3 0.0 copy-done.8
  54.3 0.6 dynamic-slice
  54.9 0.9 dynamic-update-slice
  55.7 3.3 %reshape.139 = f32[16,4,2304]{2,0,1:T(8,128)S(1)} reshape(f32[4,4,4,4,24,24]{5,4,3,1,0,2:T(8,128)} %maximum_bitcast_fusion) | data formatting | bytes 1179648 | tf_op jit(solution)/shard_map/reshape | solution.py:27
  59.0 13.8 %all-reduce.2 = s32[16]{0:T(128)S(1)} all-reduce(s32[16]{0:T(128)S(1)} %dynamic-update-slice), channel_id=1, replica_groups=mesh['group'=2,'patch'=16] {'patch'}, use_global_device_ids=true, to_apply=%add.2 | all-reduce | flops 16 | bytes 128
  73.5 0.2 select_reduce_fusion
  73.7 0.4 fusion.78
  74.1 0.4 copy.36
  74.5 19.8 %all_to_all.5 = f32[16,4,2304]{2,1,0:T(4,128)S(1)} all-to-all(f32[16,4,2304]{2,1,0:T(4,128)S(1)} %copy.36), channel_id=1, replica_groups=mesh['group'=2,'patch'=16] {'patch'}, dimensions={0} | all-to-all | bytes 1179648 | tf_op jit(solution)/shard_map/all_to_all | solution.py:105
  94.3 0.7 reduce_sum.19
  95.0 0.0 copy-done.1
  (7 shorter events, 0.2 us)
Async XLA Ops:
  0.0 2.1 %copy-start = (bf16[1,64,4,2304]{3,2,1,0:T(4,128)(2,1)S(1)}, bf16[1,64,4,2304]{3,2,1,0:T(4,128)(2,1)}, u32[]{:S(2)}) copy-start(bf16[1,64,4,2304]{3,2,1,0:T(4,128)(2,1)} %param.8) | copy-start | bytes 3538948
  13.1 7.6 %copy-start.3 = (bf16[9216]{0:T(1024)(128)(2,1)S(1)}, bf16[9216]{0:T(1024)(128)(2,1)}, u32[]{:S(2)}) copy-start(bf16[9216]{0:T(1024)(128)(2,1)} %fusion.46) | copy-start | bytes 55300
  13.1 7.6 %copy-start.5 = (bf16[9,28,28]{2,1,0:T(8,128)(2,1)S(1)}, bf16[9,28,28]{2,1,0:T(8,128)(2,1)}, u32[]{:S(2)}) copy-start(bf16[9,28,28]{2,1,0:T(8,128)(2,1)} %param.10) | copy-start | bytes 42340
  21.8 1.3 %copy-start.4 = (bf16[9216]{0:T(1024)(128)(2,1)S(1)}, bf16[9216]{0:T(1024)(128)(2,1)}, u32[]{:S(2)}) copy-start(bf16[9216]{0:T(1024)(128)(2,1)} %fusion.47) | copy-start | bytes 55300
  23.1 2.9 %slice-start = ((s8[9437184]{0:T(1024)(128)(4,1)}), s8[4194304]{0:T(1024)(128)(4,1)S(1)}, s32[]{:S(2)}) async-start(s8[9437184]{0:T(1024)(128)(4,1)} %bitcast.101), calls=%async_computation.1 | async-start | bytes 8388608
  23.1 3.5 %slice-start.1 = ((s8[9437184]{0:T(1024)(128)(4,1)}), s8[4194304]{0:T(1024)(128)(4,1)S(1)}, s32[]{:S(2)}) async-start(s8[9437184]{0:T(1024)(128)(4,1)} %bitcast.101), calls=%async_computation.2 | async-start | bytes 8388608
  24.6 2.5 %slice-start.2 = ((s8[9437184]{0:T(1024)(128)(4,1)}), s8[1048576]{0:T(1024)(128)(4,1)S(1)}, s32[]{:S(2)}) async-start(s8[9437184]{0:T(1024)(128)(4,1)} %bitcast.101), calls=%async_computation.3 | async-start | bytes 2097152
  34.5 1.9 %copy-start.6 = (bf16[3,28,28]{2,1,0:T(8,128)(2,1)S(1)}, bf16[3,28,28]{2,1,0:T(8,128)(2,1)}, u32[]{:S(2)}) copy-start(bf16[3,28,28]{2,1,0:T(8,128)(2,1)} %param.11) | copy-start | bytes 14116
  36.4 1.4 %copy-start.2 = (bf16[28,4,9216]{2,0,1:T(8,128)(2,1)}, bf16[28,4,9216]{2,0,1:T(8,128)(2,1)S(1)}, u32[]{:S(2)}) copy-start(bf16[28,4,9216]{2,0,1:T(8,128)(2,1)S(1)} %fusion.6) | copy-start | bytes 6193156
  37.8 3.1 %copy-start.7 = (bf16[3,28]{1,0:T(4,128)(2,1)S(1)}, bf16[3,28]{1,0:T(4,128)(2,1)}, u32[]{:S(2)}) copy-start(bf16[3,28]{1,0:T(4,128)(2,1)} %param.12) | copy-start | bytes 508
  52.4 2.0 %copy-start.8 = (u32[32]{0:T(128)S(1)}, u32[32]{0:T(128)}, u32[]{:S(2)}) copy-start(u32[32]{0:T(128)} %constant.126) | copy-start | bytes 388
  54.9 40.1 %copy-start.1 = (bf16[1,64,4,2304]{3,2,1,0:T(4,128)(2,1)S(1)}, bf16[1,64,4,2304]{3,2,1,0:T(4,128)(2,1)}, u32[]{:S(2)}) copy-start(bf16[1,64,4,2304]{3,2,1,0:T(4,128)(2,1)} %param.8) | copy-start | bytes 3538948
where the time goes:
time: 95.4 us; the launch traced here: 95 us
  blocking collectives  33.6 us (35%)
  local copies, waits for them, and re-layouts  27.7 us (29%)
  matrix products  25.6 us (27%)
  other arithmetic  5.69 us (6%)
  between operations  2.36 us (2%)
    all_to_all x1, blocking collectives, on_device(): lax.all_to_all(departing_pieces, 'patch', split_axis=0, concat_axis=0, ti...  19.8 us
    dot_general x9, matrix products, patch_output(): jnp.einsum('oi,izp->ozp', w_plane[3 * row_tap + col_tap], shifted_in, pre...  14.6 us
    unnamed x1, blocking collectives  13.8 us
    broadcast_in_dim x2, local copies, waits for them, and re-layouts, patch_output(): jnp.broadcast_to(coarse_grid, (hidden, patch_depth, half_side, 2, half_si...  9.15 us
    reshape x1, local copies, waits for them, and re-layouts, patch_output(): upsampled = upsampled.reshape(hidden, patch_depth, plane_side * plane_side)  7.54 us
    dot_general x1, matrix products, patch_output(): jnp.einsum('oi,izp->ozp', w_head, second_out, preferred_element_type=jnp....  4.8 us
    dot_general x2, matrix products, patch_output(): jnp.einsum('oi,izp->ozp', w_depth[depth_tap], padded_depth[:, depth_tap:d...  4.02 us
    reshape x1, local copies, waits for them, and re-layouts, brick_partition(): return blocks.reshape(16, channels, patch_depth * brick_side * brick_side)  3.29 us

commit v1 on v0

v1 whole, which is shorter than its diff:
```python
import functools
import math

import numpy as np

import jax
import jax.numpy as jnp
from jax import lax
from jax.experimental import pallas as pl
from jax.experimental.pallas import tpu as pltpu
from jax.sharding import PartitionSpec as P

F32 = jnp.float32
BF16 = jnp.bfloat16
I32 = jnp.int32
PAD = 32
LANES = 128


def iota(shape, axis):
    return lax.broadcasted_iota(I32, shape, axis)


def vmem():
    return pl.BlockSpec(memory_space=pltpu.VMEM)


def smem():
    return pl.BlockSpec(memory_space=pltpu.SMEM)


def params():
    return pltpu.CompilerParams(vmem_limit_bytes=24 * 2**20)


def bump(length):
    position = (np.arange(length, dtype=np.float64) + 0.5) / length
    return 0.1 + np.sin(np.pi * position) ** 2


def weights_kernel(aug_ref, w_in_ref, w_plane_ref, w_depth_ref, w_head_ref, big_ref, plane_ref, depth_ref, head_ref, plane_scr, depth_scr):
    hidden, _ = w_in_ref.shape
    depth = depth_ref.shape[0] // PAD
    maps = w_head_ref.shape[0]
    aug = aug_ref[0]
    zf, yf, xf = aug & 1, (aug >> 1) & 1, (aug >> 2) & 1

    rows, cols = big_ref.shape
    spread = (iota((rows, hidden), 0) % PAD == iota((rows, hidden), 1)).astype(BF16)
    gather = (iota((w_in_ref.shape[1], cols), 1) // depth == iota((w_in_ref.shape[1], cols), 0)).astype(BF16)
    tall = jnp.dot(spread, w_in_ref[...], preferred_element_type=F32).astype(BF16)
    wide = jnp.dot(tall, gather, preferred_element_type=F32)
    same = iota((rows, cols), 1) % depth == iota((rows, cols), 0) // PAD
    big_ref[...] = jnp.where(same, wide, 0.0).astype(BF16)

    plane_scr[...] = jnp.zeros_like(plane_scr)
    taps = [w_plane_ref[t].astype(F32) for t in range(9)]
    near = (((0,), (1, 2), ()), ((), (0, 1), (2,)))
    for py in range(2):
        for px in range(2):
            for dy in range(2):
                for dx in range(3):
                    hit = [taps[3 * ty + tx] for ty in near[py][dy + py] for tx in near[px][dx]]
                    if not hit:
                        continue
                    total = functools.reduce(lambda a, b: a + b, hit)
                    high = total.astype(BF16).astype(F32)
                    col = (3 * dy + dx) * PAD
                    plane_scr[py, pl.ds(px * PAD, hidden), pl.ds(col, hidden)] = high
                    plane_scr[py, pl.ds((2 + px) * PAD, hidden), pl.ds(col, hidden)] = total - high
    plane_ref[...] = plane_scr[...].astype(BF16)

    depth_scr[...] = jnp.zeros_like(depth_scr)
    for t in range(3):
        tap = w_depth_ref[t].astype(F32)
        for z in range(depth):
            if 0 <= z + t - 1 < depth:
                depth_scr[pl.ds(z * PAD, hidden), pl.ds((z + t - 1) * PAD, hidden)] = tap
    depth_ref[...] = depth_scr[...].astype(BF16)

    rows, cols = head_ref.shape
    pick = (iota((rows, maps), 0) % maps == iota((rows, maps), 1)).astype(BF16)
    tall = jnp.dot(pick, w_head_ref[...], preferred_element_type=F32).astype(BF16)
    gather = (iota((hidden, cols), 1) % PAD == iota((hidden, cols), 0)).astype(BF16)
    wide = jnp.dot(tall, gather, preferred_element_type=F32)
    at = iota((rows, cols), 0) // maps
    came = iota((rows, cols), 1) // PAD
    flip = (2 * yf + xf) * depth + (depth - 1) * zf
    head_ref[...] = jnp.where(at == (came ^ flip), wide, 0.0).astype(BF16)


def pack_weights(aug_code, w_in, w_plane, w_depth, w_head, depth):
    hidden, channels = w_in.shape
    maps = w_head.shape[0]
    shapes = (
        (depth * PAD, channels * depth),
        (2, 4 * PAD, 6 * PAD),
        (depth * PAD, depth * PAD),
        (4 * depth * maps, 4 * depth * PAD),
    )
    return pl.pallas_call(
        weights_kernel,
        out_shape=[jax.ShapeDtypeStruct(s, BF16) for s in shapes],
        in_specs=[smem()] + [vmem()] * 4,
        out_specs=[vmem()] * 4,
        scratch_shapes=[pltpu.VMEM(shapes[1], F32), pltpu.VMEM(shapes[2], F32)],
        compiler_params=params(),
        name="weights",
    )(aug_code, w_in, w_plane, w_depth, w_head)


def patch_kernel(half, aug_ref, x_ref, big_ref, plane_ref, depth_ref, head_ref, out_ref, xs_ref, a_ref):
    channels, depth, cells = x_ref.shape
    rows = depth * PAD
    step = 2 * LANES
    margin = LANES
    aug = aug_ref[0]
    yf, xf = (aug >> 1) & 1, (aug >> 2) & 1

    x = x_ref[...].reshape(channels * depth, cells)
    projected = jnp.dot(big_ref[...], x, preferred_element_type=F32).astype(BF16)
    zeros = jnp.zeros((rows, margin), BF16)
    padded = jnp.concatenate([zeros, projected, zeros], axis=1)
    column = iota((rows, cells), 1) % half
    for d in range(3):
        shifted = projected if d == 1 else lax.slice_in_dim(padded, margin + d - 1, margin + d - 1 + cells, axis=1)
        if d == 0:
            shifted = jnp.where(column == 0, jnp.zeros_like(shifted), shifted)
        if d == 2:
            shifted = jnp.where(column == half - 1, jnp.zeros_like(shifted), shifted)
        xs_ref[d, :, pl.ds(0, margin)] = zeros
        xs_ref[d, :, pl.ds(margin, cells)] = shifted
        xs_ref[d, :, pl.ds(margin + cells, margin)] = zeros

    for t in range(cells // step):
        near = []
        for d in range(3):
            block = xs_ref[d, :, pl.ds(t * step, step + 2 * margin)]
            near.append([lax.slice_in_dim(block, margin + half * e, margin + half * e + step, axis=1) for e in (-1, 0, 1)])
        centre = near[1][1].astype(F32)
        first = [[None] * depth for _ in range(4)]
        for z in range(depth):
            cut = slice(z * PAD, (z + 1) * PAD)
            for py in range(2):
                around = jnp.concatenate([near[d][py + e][cut] for e in range(2) for d in range(3)], axis=0)
                mix = jnp.dot(plane_ref[py], around, preferred_element_type=F32)
                for px in range(2):
                    total = mix[px * PAD : (px + 1) * PAD] + mix[(2 + px) * PAD : (3 + px) * PAD]
                    first[2 * py + px][z] = (centre[cut] + jnp.maximum(total, 0.0)).astype(BF16)
        second = []
        for p in range(4):
            one = jnp.concatenate(first[p], axis=0)
            mix = jnp.dot(depth_ref[...], one, preferred_element_type=F32)
            second.append((one.astype(F32) + jnp.maximum(mix, 0.0)).astype(BF16))
        logits = jnp.zeros((head_ref.shape[0], step), F32)
        for q in range(2):
            pair = jnp.concatenate(second[2 * q : 2 * q + 2], axis=0)
            logits = logits + jnp.dot(head_ref[:, 2 * q * rows : 2 * (q + 1) * rows], pair, preferred_element_type=F32)
        affinity = jax.nn.sigmoid(logits)
        for u in range(step // LANES):
            a_ref[t * (step // LANES) + u] = affinity[:, u * LANES : (u + 1) * LANES]

    side = half // 4
    main, tail = LANES, side * side - LANES
    tiles = head_ref.shape[0] // 8
    lane = iota((8, LANES), 1)

    def source(cell, j, odd):
        yl = cell // side
        xl = cell - yl * side
        y = jnp.where(yf == 1, side - 1 - yl, yl)
        xx = side * j + xl
        xx = jnp.where(xf == 1, half - 1 - xx, xx)
        return y * half + xx + odd * (LANES // 2)

    span = -(-side * half // LANES)
    rest_base = jnp.where(yf == 1, 0, span - 2)
    group = lane // tail
    for odd in range(2):
        for j in range(4):
            src = source(lane, j, odd)
            tile_of, lane_of = src // LANES, src % LANES
            hits = [tile_of == k for k in range(span)]
            rest = source(LANES + lane % tail, j, odd)
            rest_hit = rest // LANES == rest_base
            rest_lane = rest % LANES
            for i in range(odd, 4, 2):
                base = side * half * i // LANES
                brick = (i ^ (3 * yf)) * 4 + j
                packed = jnp.zeros((8, LANES), F32)
                for r in range(tiles):
                    cut = pl.ds(8 * r, 8)
                    value = jnp.take_along_axis(a_ref[base, cut], lane_of, axis=1)
                    for k in range(1, span):
                        value = jnp.where(hits[k], jnp.take_along_axis(a_ref[base + k, cut], lane_of, axis=1), value)
                    out_ref[brick, cut] = value
                    low = jnp.take_along_axis(a_ref[base + rest_base, cut], rest_lane, axis=1)
                    high = jnp.take_along_axis(a_ref[base + rest_base + 1, cut], rest_lane, axis=1)
                    packed = jnp.where(group == r, jnp.where(rest_hit, low, high), packed)
                out_ref[brick, pl.ds(8 * tiles, 8)] = packed


def patch_bricks(aug_code, feat, packed):
    channels, depth, cells = feat.shape
    half = math.isqrt(cells)
    big, plane, depth_w, head = packed
    kept = head.shape[0]
    return pl.pallas_call(
        functools.partial(patch_kernel, half),
        out_shape=jax.ShapeDtypeStruct((16, kept + 8, LANES), F32),
        in_specs=[smem()] + [vmem()] * 5,
        out_specs=vmem(),
        scratch_shapes=[
            pltpu.VMEM((3, depth * PAD, cells + 2 * LANES), BF16),
            pltpu.VMEM((cells // LANES, kept, LANES), F32),
        ],
        compiler_params=params(),
        cost_estimate=pl.CostEstimate(flops=2 * 10**9, bytes_accessed=2 * 10**6, transcendentals=0),
        name="patch",
    )(aug_code, feat, big, plane, depth_w, head)


def seed_kernel(owner_ref, anchor_ref, out_ref):
    me = lax.axis_index("patch")
    kind = iota(out_ref.shape, 0)
    here = iota(out_ref.shape, 1) == me
    value = jnp.where(kind == 0, owner_ref[0], anchor_ref[0])
    out_ref[...] = jnp.where(here, value, 0)


def seed_table(owner, anchor, devices):
    width = -(-devices // LANES) * LANES
    return pl.pallas_call(
        seed_kernel,
        out_shape=jax.ShapeDtypeStruct((2, width), I32),
        in_specs=[smem(), smem()],
        out_specs=vmem(),
        compiler_params=params(),
        name="seed",
    )(owner, anchor)


def partner(devices, bit):
    return [(d, d ^ bit) for d in range(devices)]


def slots_kernel(devices, bits, table_ref, mine_ref, other_ref, window_ref, send_ref, keep_ref, place_ref):
    me = lax.axis_index("patch")
    brick_rows = devices // 4

    def note(b, _):
        place_ref[table_ref[0, b]] = b
        return 0

    lax.fori_loop(0, devices, note, 0)
    anchor = table_ref[1, me]
    count = 1 << len(bits)
    for s in range(count):
        mask = sum(bit for k, bit in enumerate(bits) if s >> (len(bits) - 1 - k) & 1)
        brick = place_ref[me ^ mask]
        row = lax.rem(brick // 4 - anchor + brick_rows, brick_rows)
        at = row * 4 + brick % 4
        if brick_rows > 4:
            at = jnp.where(row < 4, at, 0)
        value = (mine_ref[at] + other_ref[at]) * window_ref[at]
        if brick_rows > 4:
            value = jnp.where(row < 4, value, 0.0)
        if s < count // 2:
            keep_ref[s] = value
        else:
            send_ref[s - count // 2] = value


def fill_slots(devices, bits, table, mine, other, window):
    shape = jax.ShapeDtypeStruct((1 << (len(bits) - 1),) + mine.shape[1:], F32)
    return pl.pallas_call(
        functools.partial(slots_kernel, devices, bits),
        out_shape=[shape, shape],
        in_specs=[smem()] + [vmem()] * 3,
        out_specs=[vmem()] * 2,
        scratch_shapes=[pltpu.SMEM((devices,), I32)],
        compiler_params=params(),
        name="slots",
    )(table, mine, other, window)


def brick_kernel(devices, side, maps, depth_curve, table_ref, mine_ref, other_ref, rows_ref, cols_ref, out_ref):
    depth = len(depth_curve)
    wide = 2 * side
    plane = wide * wide
    tail = side * side - LANES
    per = depth * maps
    brick = mine_ref[0] + other_ref[0]
    kept = 4 * per
    main, packed = brick[:kept], brick[kept:]
    rest = jnp.concatenate([packed if k == 0 else pltpu.roll(packed, LANES - tail * k, 1) for k in range(kept // 8)], axis=0)
    fill = jnp.zeros((16 - per, LANES), F32)
    mains = [jnp.concatenate([main[per * p : per * (p + 1)], fill], axis=0) for p in range(4)]
    rests = [jnp.concatenate([rest[per * p : per * (p + 1)], fill], axis=0) for p in range(4)]
    columns = []
    for d in range(-(-plane // LANES)):
        n = iota((8, LANES), 1) + d * LANES
        y = n // wide
        x = n - y * wide
        cell = (y // 2) * side + x // 2
        quarter = 2 * (y % 2) + x % 2
        lane_of = cell % LANES
        top = min((d + 1) * LANES, plane) - 1
        tiles = []
        for r in range(2):
            cut = slice(8 * r, 8 * r + 8)
            value = None
            for p in range(4):
                one = jnp.take_along_axis(mains[p][cut], lane_of, axis=1)
                if (top // wide // 2 + 1) * side > LANES:
                    one = jnp.where(cell >= LANES, jnp.take_along_axis(rests[p][cut], lane_of, axis=1), one)
                value = one if value is None else jnp.where(quarter == p, one, value)
            tiles.append(value)
        columns.append(jnp.concatenate(tiles, axis=0))
    cells = jnp.concatenate(columns, axis=1)[:, :plane]
    for z in range(depth):
        out_ref[0, pl.ds(0, maps), pl.ds(z * plane, plane)] = cells[z * maps : (z + 1) * maps]

    me = lax.axis_index("patch")
    brick_rows = devices // 4
    owned = lax.fori_loop(0, devices, lambda b, at: jnp.where(table_ref[0, b] == me, b, at), 0)
    row, col = owned // 4, owned % 4

    def tally(d, counts):
        i = lax.rem(row - table_ref[1, d] + brick_rows, brick_rows)
        return tuple(c + jnp.where(i == k, 1, 0) for k, c in enumerate(counts))

    counts = lax.fori_loop(0, devices, tally, (0, 0, 0, 0))
    rows = sum(c.astype(F32) * rows_ref[pl.ds(k, 1), :] for k, c in enumerate(counts))
    window = (rows * cols_ref[pl.ds(col, 1), :])[:, :plane]
    for z in range(depth):
        out_ref[0, pl.ds(maps, 1), pl.ds(z * plane, plane)] = window * depth_curve[z]


def finish(devices, side, maps, depth, table, mine, other):
    plane = 4 * side * side
    width = -(-plane // LANES) * LANES
    curve = bump(8 * side)
    n = np.arange(width)
    y, x = np.minimum(n // (2 * side), 2 * side - 1), n % (2 * side)
    rows = np.stack([curve[2 * side * i + y] for i in range(4)]).astype(np.float32)
    cols = np.stack([curve[2 * side * i + x] for i in range(4)]).astype(np.float32)
    depth_curve = [float(np.float32(v)) for v in bump(depth)]
    return pl.pallas_call(
        functools.partial(brick_kernel, devices, side, maps, depth_curve),
        out_shape=jax.ShapeDtypeStruct((1, maps + 1, depth * plane), F32),
        in_specs=[smem()] + [vmem()] * 4,
        out_specs=vmem(),
        compiler_params=params(),
        name="brick",
    )(table, mine, other, rows, cols)


def wire_window(side, maps, depth):
    curve_y, curve_z = bump(8 * side), bump(depth)
    cell = np.arange(side * side)
    out = np.zeros((16, 4 * depth * maps, side * side))
    for i in range(4):
        for j in range(4):
            for p in range(4):
                y = curve_y[2 * side * i + 2 * (cell // side) + p // 2]
                x = curve_y[2 * side * j + 2 * (cell % side) + p % 2]
                for z in range(depth):
                    for m in range(maps):
                        out[4 * i + j, (p * depth + z) * maps + m] = curve_z[z] * y * x
    kept = out.shape[1]
    tail = side * side - LANES
    packed = np.zeros((16, 8, LANES))
    for k in range(kept // 8):
        packed[:, :, tail * k : tail * (k + 1)] = out[:, 8 * k : 8 * k + 8, LANES:]
    return np.concatenate([out[:, :, :LANES], packed], axis=1).astype(np.float32)


def on_device(features, w_in, w_plane, w_depth, w_head, brick_owner, patch_anchor, aug_code):
    devices = lax.axis_size("patch")
    _, _, depth, cells = features.shape
    side = math.isqrt(cells) // 4
    maps = w_head.shape[0]
    bits = [1 << k for k in range(devices.bit_length() - 1)]

    table = seed_table(brick_owner, patch_anchor, devices)
    for bit in bits:
        table = table + lax.ppermute(table, "patch", partner(devices, bit))
    packed = pack_weights(aug_code, w_in, w_plane, w_depth, w_head, depth)
    bricks = patch_bricks(aug_code, features[0], packed)
    other = lax.ppermute(bricks, "patch", partner(devices, 1))
    send, keep = fill_slots(devices, bits[1:], table, bricks, other, wire_window(side, maps, depth))
    for bit in bits[1:-1]:
        got = lax.ppermute(send, "patch", partner(devices, bit))
        half = send.shape[0] // 2
        keep, send = keep[:half] + got[:half], keep[half:] + got[half:]
    other = lax.ppermute(send, "patch", partner(devices, bits[-1]))
    return finish(devices, side, maps, depth, table, keep, other)


def solution(mesh):
    one = P(("group", "patch"))
    in_specs = (P(("group", "patch"), None, None, None), P(), P(), P(), P(), one, one, one)
    return jax.shard_map(
        on_device, mesh=mesh, in_specs=in_specs, out_specs=P(("group", "patch"), None, None), check_vma=False
    )
```

time: 95.4 us -> 43.5 us (0.46)
  blocking collectives: 33.6 us -> 0 us
  matrix products: 25.6 us -> 0 us
  local copies, waits for them, and re-layouts: 27.7 us -> 4.28 us
  starting transfers between devices: 0 us -> 15.3 us
  waiting for transfers between devices: 0 us -> 12.9 us
  Pallas kernels: 0 us -> 8.63 us
  other arithmetic: 5.69 us -> 0.04 us
    dot_general x14 -> x0, matrix products: 25.6 us -> none  [the longest x9 14.6 us: patch_output(): jnp.einsum('oi,izp->ozp', w_plane[3 * row_tap + col_tap], shifted_in, pre...]
    all_to_all x1 -> x0, blocking collectives: 19.8 us -> none  [on_device(): lax.all_to_all(departing_pieces, 'patch', split_axis=0, concat_axis=0, ti...]
    ppermute x0 -> x8, starting transfers between devices: none -> 15.3 us  [the longest x4 7.86 us: on_device(): table = table + lax.ppermute(table, 'patch', partner(devices, bit))]
    unnamed x1 -> x0, blocking collectives: 13.8 us -> none
    ppermute x0 -> x8, waiting for transfers between devices: none -> 12.9 us  [the longest x4 5.8 us: on_device(): table = table + lax.ppermute(table, 'patch', partner(devices, bit))]
    reshape x3 -> x0, local copies, waits for them, and re-layouts: 11.2 us -> none  [the longest x1 7.54 us: patch_output(): upsampled = upsampled.reshape(hidden, patch_depth, plane_side * plane_side)]
    broadcast_in_dim x2 -> x0, local copies, waits for them, and re-layouts: 9.15 us -> none  [patch_output(): jnp.broadcast_to(coarse_grid, (hidden, patch_depth, half_side, 2, half_si...]
    pallas_call x0 -> x5, Pallas kernels: none -> 8.63 us  [the longest x1 5.6 us: patch_bricks(): pl.pallas_call(functools.partial(patch_kernel, half), out_shape=jax.Shape...]
  transfers between devices with their start and end apart: 0 -> 8, of which waited for: 0 -> 7; matrix products, arithmetic and copies ran while one was open for 0% -> 0% of each run, Pallas kernels for 0% -> 0%
where the time goes in v1:
time: 43.5 us; the launch traced here: 43.1 us
  starting transfers between devices  15.3 us (35%)
  waiting for transfers between devices  12.9 us (30%)
  Pallas kernels  8.63 us (20%)
  local copies, waits for them, and re-layouts  4.28 us (10%)
  between operations  2.02 us (5%)
    ppermute x4, starting transfers between devices, on_device(): table = table + lax.ppermute(table, 'patch', partner(devices, bit))  7.86 us
    ppermute x4, waiting for transfers between devices, on_device(): table = table + lax.ppermute(table, 'patch', partner(devices, bit))  5.8 us
    pallas_call x1, Pallas kernels, patch_bricks(): pl.pallas_call(functools.partial(patch_kernel, half), out_shape=jax.Shape...  5.6 us
    ppermute x2, waiting for transfers between devices, on_device(): got = lax.ppermute(send, 'patch', partner(devices, bit))  5.2 us
    unnamed x16, local copies, waits for them, and re-layouts  4.28 us
    ppermute x2, starting transfers between devices, on_device(): got = lax.ppermute(send, 'patch', partner(devices, bit))  3.9 us
    ppermute x1, starting transfers between devices, on_device(): other = lax.ppermute(send, 'patch', partner(devices, bits[-1]))  2.99 us
    ppermute x1, waiting for transfers between devices, on_device(): other = lax.ppermute(send, 'patch', partner(devices, bits[-1]))  1.85 us
  transfers between devices with their start and end apart: 8, of which 7 were waited for; matrix products, arithmetic and copies ran while one was open for 0% of the time, Pallas kernels for 0%

profile of v1, /device:TPU:0, one launch (start us, length us, event | category | flops | bytes accessed | tf_op | source)
XLA Modules:
  0.0 43.1 jit_solution(17429462387258832346)
XLA Ops:
  0.7 0.0 copy-start.1
  0.7 0.9 %copy-done.1 = bf16[9,28,28]{2,1,0:T(8,128)(2,1)S(1)} copy-done((bf16[9,28,28]{2,1,0:T(8,128)(2,1)S(1)}, bf16[9,28,28]{2,1,0:T(8,128)(2,1)}, u32[]{:S(2)}) %copy-start.1) | copy-done | bytes 14136
  1.5 0.0 copy-start.2
  1.5 0.7 %copy-done.2 = bf16[3,28,28]{2,1,0:T(8,128)(2,1)S(1)} copy-done((bf16[3,28,28]{2,1,0:T(8,128)(2,1)S(1)}, bf16[3,28,28]{2,1,0:T(8,128)(2,1)}, u32[]{:S(2)}) %copy-start.2) | copy-done | bytes 4728
  2.3 0.0 copy-start.5
  2.3 0.7 %copy-done.5 = bf16[28,64]{1,0:T(8,128)(2,1)S(1)} copy-done((bf16[28,64]{1,0:T(8,128)(2,1)S(1)}, bf16[28,64]{1,0:T(8,128)(2,1)}, u32[]{:S(2)}) %copy-start.5) | copy-done | bytes 3608
  3.0 0.0 copy-start.6
  3.0 0.7 %copy-done.6 = bf16[3,28]{1,0:T(4,128)(2,1)S(1)} copy-done((bf16[3,28]{1,0:T(4,128)(2,1)S(1)}, bf16[3,28]{1,0:T(4,128)(2,1)}, u32[]{:S(2)}) %copy-start.6) | copy-done | bytes 192
  3.7 0.4 weights.1
  4.0 0.0 copy-start.7
  4.0 1.3 %copy-done.7 = bf16[1,64,4,2304]{3,2,1,0:T(4,128)(2,1)S(1)} copy-done((bf16[1,64,4,2304]{3,2,1,0:T(4,128)(2,1)S(1)}, bf16[1,64,4,2304]{3,2,1,0:T(4,128)(2,1)}, u32[]{:S(2)}) %copy-start.7) | copy-done | bytes 1179672
  5.3 0.0 copy-start
  5.3 5.6 %patch.1.mine_ref = f32[16,56,128]{2,1,0:T(8,128)S(1)} custom-call(s32[1]{0:T(128)S(6)} %copy.14.aug_ref, bf16[64,4,2304]{2,1,0:T(4,128)(2,1)S(1)} %bitcast.1, bf16[128,256]{1,0:T(8,128)(2,1)S(1)} %get-tuple-element.11.big_ref, bf16[2,128,192]{2,1,0:T(8,128)(2,1)S(1)} %get-tuple-element.12.plane_ref, bf16[128,128]{1,0:T(8,128)(2,1)S(1)} %get-tuple-element.13.depth_ref, ...), custom_call_target="tpu_custom_call" | custom-call | flops 2000000000 | bytes 2000000 | tf_op jit(solution)/shard_map/patch/pallas_call | solution.py:208
  10.9 0.0 copy-start.3
  10.9 0.0 copy-start.4
  10.9 0.6 %collective-permute-start.4 = (f32[16,56,128]{2,1,0:T(8,128)S(1)}, f32[16,56,128]{2,1,0:T(8,128)S(1)}, u32[]{:S(2)}, u32[]{:S(2)}) collective-permute-start(f32[16,56,128]{2,1,0:T(8,128)S(1)} %patch.1.mine_ref), channel_id=1, source_target_pairs={{0,1},{1,0},{2,3},{3,2},{4,5},{5,4},{6,7},{7,6},{8,9},{9,8},{10,11... | collective-permute-start | bytes 1376264 | tf_op jit(solution)/shard_map/ppermute | solution.py:391
  12.8 0.1 collective-permute-start
  12.9 1.1 %collective-permute-done = s32[2,128]{1,0:T(2,128)S(1)} collective-permute-done((s32[2,128]{1,0:T(2,128)S(1)}, s32[2,128]{1,0:T(2,128)S(1)}, u32[]{:S(2)}, u32[]{:S(2)}) %collective-permute-start) | collective-permute-done | bytes 1056 | tf_op jit(solution)/shard_map/ppermute | solution.py:388
  14.1 2.7 %collective-permute-start.1 = (s32[2,128]{1,0:T(2,128)S(1)}, s32[2,128]{1,0:T(2,128)S(1)}, u32[]{:S(2)}, u32[]{:S(2)}) collective-permute-start(s32[2,128]{1,0:T(2,128)S(1)} %add.24), channel_id=1, source_target_pairs={{0,2},{1,3},{2,0},{3,1},{4,6},{5,7},{6,4},{7,5},{8,10},{9,11},{10,... | collective-permute-start | bytes 3080 | tf_op jit(solution)/shard_map/ppermute | solution.py:388
  16.7 1.6 %collective-permute-done.1 = s32[2,128]{1,0:T(2,128)S(1)} collective-permute-done((s32[2,128]{1,0:T(2,128)S(1)}, s32[2,128]{1,0:T(2,128)S(1)}, u32[]{:S(2)}, u32[]{:S(2)}) %collective-permute-start.1) | collective-permute-done | bytes 1056 | tf_op jit(solution)/shard_map/ppermute | solution.py:388
  18.3 2.1 %collective-permute-start.2 = (s32[2,128]{1,0:T(2,128)S(1)}, s32[2,128]{1,0:T(2,128)S(1)}, u32[]{:S(2)}, u32[]{:S(2)}) collective-permute-start(s32[2,128]{1,0:T(2,128)S(1)} %add.25), channel_id=1, source_target_pairs={{0,4},{1,5},{2,6},{3,7},{4,0},{5,1},{6,2},{7,3},{8,12},{9,13},{10,... | collective-permute-start | bytes 3080 | tf_op jit(solution)/shard_map/ppermute | solution.py:388
  20.4 1.6 %collective-permute-done.2 = s32[2,128]{1,0:T(2,128)S(1)} collective-permute-done((s32[2,128]{1,0:T(2,128)S(1)}, s32[2,128]{1,0:T(2,128)S(1)}, u32[]{:S(2)}, u32[]{:S(2)}) %collective-permute-start.2) | collective-permute-done | bytes 1056 | tf_op jit(solution)/shard_map/ppermute | solution.py:388
  21.9 3.0 %collective-permute-start.3 = (s32[2,128]{1,0:T(2,128)S(1)}, s32[2,128]{1,0:T(2,128)S(1)}, u32[]{:S(2)}, u32[]{:S(2)}) collective-permute-start(s32[2,128]{1,0:T(2,128)S(1)} %add.26), channel_id=1, source_target_pairs={{0,8},{1,9},{2,10},{3,11},{4,12},{5,13},{6,14},{7,15},{8,0},{9,1},... | collective-permute-start | bytes 3080 | tf_op jit(solution)/shard_map/ppermute | solution.py:388
  25.0 1.6 %collective-permute-done.3 = s32[2,128]{1,0:T(2,128)S(1)} collective-permute-done((s32[2,128]{1,0:T(2,128)S(1)}, s32[2,128]{1,0:T(2,128)S(1)}, u32[]{:S(2)}, u32[]{:S(2)}) %collective-permute-start.3) | collective-permute-done | bytes 1056 | tf_op jit(solution)/shard_map/ppermute | solution.py:388
  26.5 0.0 collective-permute-done.4.other_ref
  26.5 0.0 copy-done
  26.5 0.8 %slots.1 = (f32[4,56,128]{2,1,0:T(8,128)S(1)}, f32[4,56,128]{2,1,0:T(8,128)S(1)}) custom-call(s32[2,128]{1,0:T(2,128)S(1)} %add.27.table_ref, f32[16,56,128]{2,1,0:T(8,128)S(1)} %patch.1.mine_ref, f32[16,56,128]{2,1,0:T(8,128)S(1)} %collective-permute-done.4.other_ref, f32[16,56,128]{2,1,0:T(8,128)S(1)} %copy-done), custom_call_target="tpu_custom_call" | custom-call | tf_op jit(solution)/shard_map/slots/pallas_call | solution.py:276
  27.3 1.9 %collective-permute-start.5 = (f32[4,56,128]{2,1,0:T(8,128)S(1)}, f32[4,56,128]{2,1,0:T(8,128)S(1)}, u32[]{:S(2)}, u32[]{:S(2)}) collective-permute-start(f32[4,56,128]{2,1,0:T(8,128)S(1)} %get-tuple-element.16), channel_id=1, source_target_pairs={{0,2},{1,3},{2,0},{3,1},{4,6},{5,7},{6,4},{7,5},{8,10},{9,11},{10,... | collective-permute-start | bytes 344072 | tf_op jit(solution)/shard_map/ppermute | solution.py:394
  29.2 2.9 %collective-permute-done.5 = f32[4,56,128]{2,1,0:T(8,128)S(1)} collective-permute-done((f32[4,56,128]{2,1,0:T(8,128)S(1)}, f32[4,56,128]{2,1,0:T(8,128)S(1)}, u32[]{:S(2)}, u32[]{:S(2)}) %collective-permute-start.5) | collective-permute-done | bytes 114720 | tf_op jit(solution)/shard_map/ppermute | solution.py:394
  32.2 2.0 %collective-permute-start.6 = (f32[2,56,128]{2,1,0:T(8,128)S(1)}, f32[2,56,128]{2,1,0:T(8,128)S(1)}, u32[]{:S(2)}, u32[]{:S(2)}) collective-permute-start(f32[2,56,128]{2,1,0:T(8,128)S(1)} %get-tuple-element.18), channel_id=1, source_target_pairs={{0,4},{1,5},{2,6},{3,7},{4,0},{5,1},{6,2},{7,3},{8,12},{9,13},{10,... | collective-permute-start | bytes 172040 | tf_op jit(solution)/shard_map/ppermute | solution.py:394
  34.2 2.3 %collective-permute-done.6 = f32[2,56,128]{2,1,0:T(8,128)S(1)} collective-permute-done((f32[2,56,128]{2,1,0:T(8,128)S(1)}, f32[2,56,128]{2,1,0:T(8,128)S(1)}, u32[]{:S(2)}, u32[]{:S(2)}) %collective-permute-start.6) | collective-permute-done | bytes 57376 | tf_op jit(solution)/shard_map/ppermute | solution.py:394
  36.4 3.0 %collective-permute-start.7 = (f32[1,56,128]{2,1,0:T(8,128)S(1)}, f32[1,56,128]{2,1,0:T(8,128)S(1)}, u32[]{:S(2)}, u32[]{:S(2)}) collective-permute-start(f32[1,56,128]{2,1,0:T(8,128)S(1)} %get-tuple-element.19), channel_id=1, source_target_pairs={{0,8},{1,9},{2,10},{3,11},{4,12},{5,13},{6,14},{7,15},{8,0},{9,1},... | collective-permute-start | bytes 86024 | tf_op jit(solution)/shard_map/ppermute | solution.py:397
  39.4 1.9 %collective-permute-done.7.other_ref = f32[1,56,128]{2,1,0:T(8,128)S(1)} collective-permute-done((f32[1,56,128]{2,1,0:T(8,128)S(1)}, f32[1,56,128]{2,1,0:T(8,128)S(1)}, u32[]{:S(2)}, u32[]{:S(2)}) %collective-permute-start.7) | collective-permute-done | bytes 28704 | tf_op jit(solution)/shard_map/ppermute | solution.py:397
  41.3 0.0 copy-done.3
  41.3 0.0 copy-done.4
  41.3 1.8 %brick.1 = f32[1,4,2304]{2,1,0:T(4,128)} custom-call(s32[2,128]{1,0:T(2,128)S(1)} %add.27.table_ref, f32[1,56,128]{2,1,0:T(8,128)S(1)} %get-tuple-element.20.mine_ref, f32[1,56,128]{2,1,0:T(8,128)S(1)} %collective-permute-done.7.other_ref, f32[4,640]{1,0:T(4,128)S(1)} %copy-done.4, f32[4,640]{1,0:T(4,128)S(1)} %copy-done.3), custom_call_target="tpu_custom_call" | custom-call | tf_op jit(solution)/shard_map/brick/pallas_call | solution.py:349
  (7 shorter events, 0.0 us)
Async XLA Ops:
  0.7 0.9 %copy-start.1 = (bf16[9,28,28]{2,1,0:T(8,128)(2,1)S(1)}, bf16[9,28,28]{2,1,0:T(8,128)(2,1)}, u32[]{:S(2)}) copy-start(bf16[9,28,28]{2,1,0:T(8,128)(2,1)} %w_plane_ref.1) | copy-start | bytes 42340
  1.5 0.7 %copy-start.2 = (bf16[3,28,28]{2,1,0:T(8,128)(2,1)S(1)}, bf16[3,28,28]{2,1,0:T(8,128)(2,1)}, u32[]{:S(2)}) copy-start(bf16[3,28,28]{2,1,0:T(8,128)(2,1)} %w_depth_ref.1) | copy-start | bytes 14116
  2.3 0.7 %copy-start.5 = (bf16[28,64]{1,0:T(8,128)(2,1)S(1)}, bf16[28,64]{1,0:T(8,128)(2,1)}, u32[]{:S(2)}) copy-start(bf16[28,64]{1,0:T(8,128)(2,1)} %w_in_ref.1) | copy-start | bytes 10756
  3.0 0.7 %copy-start.6 = (bf16[3,28]{1,0:T(4,128)(2,1)S(1)}, bf16[3,28]{1,0:T(4,128)(2,1)}, u32[]{:S(2)}) copy-start(bf16[3,28]{1,0:T(4,128)(2,1)} %w_head_ref.1) | copy-start | bytes 508
  4.0 1.3 %copy-start.7 = (bf16[1,64,4,2304]{3,2,1,0:T(4,128)(2,1)S(1)}, bf16[1,64,4,2304]{3,2,1,0:T(4,128)(2,1)}, u32[]{:S(2)}) copy-start(bf16[1,64,4,2304]{3,2,1,0:T(4,128)(2,1)} %param.11) | copy-start | bytes 3538948
  5.3 21.2 %copy-start = (f32[16,56,128]{2,1,0:T(8,128)S(1)}, f32[16,56,128]{2,1,0:T(8,128)}, u32[]{:S(2)}) copy-start(f32[16,56,128]{2,1,0:T(8,128)} %constant.6.clone.window_ref) | copy-start | bytes 1376260
  10.9 30.4 %copy-start.3 = (f32[4,640]{1,0:T(4,128)S(1)}, f32[4,640]{1,0:T(4,128)}, u32[]{:S(2)}) copy-start(f32[4,640]{1,0:T(4,128)} %constant.8.clone.cols_ref) | copy-start | bytes 30724
  10.9 30.4 %copy-start.4 = (f32[4,640]{1,0:T(4,128)S(1)}, f32[4,640]{1,0:T(4,128)}, u32[]{:S(2)}) copy-start(f32[4,640]{1,0:T(4,128)} %constant.7.clone.rows_ref) | copy-start | bytes 30724
  10.9 15.6 %collective-permute-start.4 = (f32[16,56,128]{2,1,0:T(8,128)S(1)}, f32[16,56,128]{2,1,0:T(8,128)S(1)}, u32[]{:S(2)}, u32[]{:S(2)}) collective-permute-start(f32[16,56,128]{2,1,0:T(8,128)S(1)} %patch.1.mine_ref), channel_id=1, source_target_pairs={{0,1},{1,0},{2,3},{3,2},{4,5},{5,4},{6,7},{7,6},{8,9},{9,8},{10,11... | collective-permute-start | bytes 1376264 | tf_op jit(solution)/shard_map/ppermute | solution.py:391
  12.8 1.2 %collective-permute-start = (s32[2,128]{1,0:T(2,128)S(1)}, s32[2,128]{1,0:T(2,128)S(1)}, u32[]{:S(2)}, u32[]{:S(2)}) collective-permute-start(s32[2,128]{1,0:T(2,128)S(1)} %seed.1), channel_id=1, source_target_pairs={{0,1},{1,0},{2,3},{3,2},{4,5},{5,4},{6,7},{7,6},{8,9},{9,8},{10,11... | collective-permute-start | bytes 3080 | tf_op jit(solution)/shard_map/ppermute | solution.py:388
  14.1 4.2 %collective-permute-start.1 = (s32[2,128]{1,0:T(2,128)S(1)}, s32[2,128]{1,0:T(2,128)S(1)}, u32[]{:S(2)}, u32[]{:S(2)}) collective-permute-start(s32[2,128]{1,0:T(2,128)S(1)} %add.24), channel_id=1, source_target_pairs={{0,2},{1,3},{2,0},{3,1},{4,6},{5,7},{6,4},{7,5},{8,10},{9,11},{10,... | collective-permute-start | bytes 3080 | tf_op jit(solution)/shard_map/ppermute | solution.py:388
  18.3 3.6 %collective-permute-start.2 = (s32[2,128]{1,0:T(2,128)S(1)}, s32[2,128]{1,0:T(2,128)S(1)}, u32[]{:S(2)}, u32[]{:S(2)}) collective-permute-start(s32[2,128]{1,0:T(2,128)S(1)} %add.25), channel_id=1, source_target_pairs={{0,4},{1,5},{2,6},{3,7},{4,0},{5,1},{6,2},{7,3},{8,12},{9,13},{10,... | collective-permute-start | bytes 3080 | tf_op jit(solution)/shard_map/ppermute | solution.py:388
  21.9 4.6 %collective-permute-start.3 = (s32[2,128]{1,0:T(2,128)S(1)}, s32[2,128]{1,0:T(2,128)S(1)}, u32[]{:S(2)}, u32[]{:S(2)}) collective-permute-start(s32[2,128]{1,0:T(2,128)S(1)} %add.26), channel_id=1, source_target_pairs={{0,8},{1,9},{2,10},{3,11},{4,12},{5,13},{6,14},{7,15},{8,0},{9,1},... | collective-permute-start | bytes 3080 | tf_op jit(solution)/shard_map/ppermute | solution.py:388
  27.3 4.9 %collective-permute-start.5 = (f32[4,56,128]{2,1,0:T(8,128)S(1)}, f32[4,56,128]{2,1,0:T(8,128)S(1)}, u32[]{:S(2)}, u32[]{:S(2)}) collective-permute-start(f32[4,56,128]{2,1,0:T(8,128)S(1)} %get-tuple-element.16), channel_id=1, source_target_pairs={{0,2},{1,3},{2,0},{3,1},{4,6},{5,7},{6,4},{7,5},{8,10},{9,11},{10,... | collective-permute-start | bytes 344072 | tf_op jit(solution)/shard_map/ppermute | solution.py:394
  32.2 4.2 %collective-permute-start.6 = (f32[2,56,128]{2,1,0:T(8,128)S(1)}, f32[2,56,128]{2,1,0:T(8,128)S(1)}, u32[]{:S(2)}, u32[]{:S(2)}) collective-permute-start(f32[2,56,128]{2,1,0:T(8,128)S(1)} %get-tuple-element.18), channel_id=1, source_target_pairs={{0,4},{1,5},{2,6},{3,7},{4,0},{5,1},{6,2},{7,3},{8,12},{9,13},{10,... | collective-permute-start | bytes 172040 | tf_op jit(solution)/shard_map/ppermute | solution.py:394
  36.4 4.8 %collective-permute-start.7 = (f32[1,56,128]{2,1,0:T(8,128)S(1)}, f32[1,56,128]{2,1,0:T(8,128)S(1)}, u32[]{:S(2)}, u32[]{:S(2)}) collective-permute-start(f32[1,56,128]{2,1,0:T(8,128)S(1)} %get-tuple-element.19), channel_id=1, source_target_pairs={{0,8},{1,9},{2,10},{3,11},{4,12},{5,13},{6,14},{7,15},{8,0},{9,1},... | collective-permute-start | bytes 86024 | tf_op jit(solution)/shard_map/ppermute | solution.py:397
